TPU v7x, 32 devices: a whole 2x2x4 slice. The times are simulated.
32 devices in a mesh: batch: 16 (over z, y, core), rep: 2 (over x).
Axes of the slice: x: 2, y: 2, z: 4, core: 2. Of those that a mesh axis runs over, the one named last changes fastest.
Arguments:
- image_embed: bfloat16 [2048, 1024], P('batch'), may hold values from -2 to 2
- text_embed: bfloat16 [2048, 1024], P(('batch', 'rep')), may hold values from -2 to 2
- logit_scale: float32 [1], replicated, may hold values from 50 to 100
Outputs:
- mean_loss: float32 [], replicated
- image_grad: float32 [2048, 1024], P(('batch', 'rep'))
- text_grad: float32 [2048, 1024], P(('batch', 'rep'))
All inputs are finite; a program needn't handle non-finite values.
Results may differ from a plain program's by a relative error of at most 0.0025.
Values may be sent and summed in bfloat16 or wider, within the bound.
A program may use at most 128 MiB of HBM per device.

v0:
```python
import jax
import jax.numpy as jnp
from jax import lax
from jax.sharding import PartitionSpec as P


def merged(value, axis, join):
    pieces = jax.tree.map(lambda part: lax.all_gather(part, axis), value)
    head = jax.tree.map(lambda part: part[0], pieces)
    tail = jax.tree.map(lambda part: part[1:], pieces)
    total, _ = lax.scan(lambda total, share: (join(total, share), None), head, tail)
    return total


def combine_lse(earlier, later):
    biggest = jnp.maximum(earlier[0], later[0])
    return (
        biggest,
        earlier[1] * jnp.exp(earlier[0] - biggest) + later[1] * jnp.exp(later[0] - biggest),
    )


def body(image_embed, text_embed, logit_scale):
    scale_value = logit_scale[0]
    row_count = image_embed.shape[0]
    half_rows = text_embed.shape[0]
    batch_count = lax.axis_size("batch")
    batch_index = lax.axis_index("batch")
    rep_index = lax.axis_index("rep")
    whole_text = lax.all_gather(text_embed, "batch", axis=0, tiled=True)
    scores = scale_value * lax.dot_general(
        image_embed, whole_text, (((1,), (1,)), ((), ())), preferred_element_type=jnp.float32
    )
    row_max = jnp.max(scores, axis=1)
    row_sum = jnp.sum(jnp.exp(scores - row_max[:, None]), axis=1)
    row_max, row_sum = merged((row_max, row_sum), "rep", combine_lse)
    row_lse = row_max + jnp.log(row_sum)
    column_max = jnp.max(scores, axis=0)
    column_sum = jnp.sum(jnp.exp(scores - column_max[None, :]), axis=0)
    peer_maxes, peer_sums = (
        lax.all_to_all(
            column_max.reshape(batch_count, half_rows),
            "batch",
            split_axis=0,
            concat_axis=0,
            tiled=True,
        ),
        lax.all_to_all(
            column_sum.reshape(batch_count, half_rows),
            "batch",
            split_axis=0,
            concat_axis=0,
            tiled=True,
        ),
    )
    column_top = jnp.max(peer_maxes, axis=0)
    own_lse = column_top + jnp.log(
        jnp.sum(peer_sums * jnp.exp(peer_maxes - column_top[None, :]), axis=0)
    )
    col_lse = lax.all_gather(own_lse, "batch", axis=0, tiled=True)
    own_scores = lax.dynamic_slice(
        scores, (rep_index * half_rows, batch_index * half_rows), (half_rows, half_rows)
    )
    own_diag = jnp.diagonal(own_scores)
    own_rows = lax.dynamic_slice_in_dim(row_lse, rep_index * half_rows, half_rows, 0)
    loss_sum = lax.psum(jnp.sum(own_rows + own_lse - 2.0 * own_diag), ("batch", "rep"))
    mean_loss = loss_sum / (2 * row_count * batch_count)
    row_ids = lax.broadcasted_iota(jnp.int32, scores.shape, 0) - rep_index * half_rows
    column_ids = lax.broadcasted_iota(jnp.int32, scores.shape, 1) - batch_index * half_rows
    diag_match = ((row_ids == column_ids) & (column_ids >= 0) & (column_ids < half_rows)).astype(
        jnp.float32
    )
    weights = (
        jnp.exp(scores - row_lse[:, None]) + jnp.exp(scores - col_lse[None, :]) - 2.0 * diag_match
    ).astype(jnp.bfloat16)
    image_part = (
        scale_value * 0.5 * jnp.dot(weights, whole_text, preferred_element_type=jnp.float32)
    )
    image_grad = lax.psum_scatter(image_part, "rep", scatter_dimension=0, tiled=True)
    all_rows_lse = lax.all_gather(row_lse, "batch", axis=0, tiled=True)
    own_first = (2 * batch_index + rep_index) * half_rows
    fragment = lax.all_gather(image_embed, "batch", axis=0, tiled=True)
    scores_back = scale_value * lax.dot_general(
        text_embed, fragment, (((1,), (1,)), ((), ())), preferred_element_type=jnp.float32
    )
    image_ids = lax.broadcasted_iota(jnp.int32, scores_back.shape, 1)
    text_ids = own_first + lax.broadcasted_iota(jnp.int32, scores_back.shape, 0)
    back_match = (image_ids == text_ids).astype(jnp.float32)
    weights_block = (
        jnp.exp(scores_back - own_lse[:, None])
        + jnp.exp(scores_back - all_rows_lse[None, :])
        - 2.0 * back_match
    ).astype(jnp.bfloat16)
    summed = jnp.dot(weights_block, fragment, preferred_element_type=jnp.float32)
    text_grad = scale_value * 0.5 * summed
    return (mean_loss, image_grad, text_grad)


def solution(mesh):
    in_specs = (P("batch", None), P(("batch", "rep"), None), P())
    out_specs = (P(), P(("batch", "rep"), None), P(("batch", "rep"), None))
    return jax.shard_map(body, mesh=mesh, in_specs=in_specs, out_specs=out_specs, check_vma=False)
```

profile of v0, /device:TPU:12, one launch (start us, length us, event | category | flops | bytes accessed | tf_op | source)
XLA Modules:
  0.0 189.0 jit_solution(3406999537041525352)
XLA Ops:
  7.2 0.0 all-gather.8.cloned.1.call-start
  7.2 0.7 all-gather.8.cloned.1.call-update
  7.9 0.0 copy-start
  7.9 0.0 all-gather.10.cloned.1.call-start
  8.0 0.7 all-gather.10.cloned.1.call-update
  9.3 1.2 dynamic-slice
  11.2 39.5 %all-gather.8.cloned.1.call-done = bf16[1024,1024]{1,0:T(8,128)(2,1)} async-done(((bf16[64,1024]{1,0:T(8,128)(2,1)}), bf16[1024,1024]{1,0:T(8,128)(2,1)}) %all-gather.8.cloned.1.call-update) | async-done | bytes 2097168 | tf_op jit(solution)/shard_map/all_gather | solution.py:30
  50.8 2.6 %fusion.24 = (f32[128]{0:T(128)S(1)}, f32[1024]{0:T(1024)S(1)}, f32[128,1024]{1,0:T(8,128)S(1)}) fusion(bf16[128,1024]{1,0:T(8,128)(2,1)} %param.3, bf16[1024,1024]{1,0:T(8,128)(2,1)} %all-gather.8.cloned.1.call-done, f32[]{:T(128)} %bitcast.40), kind=kOutput, calls=%fused_computation.47 | convolution fusion | flops 268827520 | bytes 2888196 | tf_op jit(solution)/shard_map/dot_general | solution.py:31
  53.4 0.7 all_to_all.16
  54.1 5.8 %all-to-all-start = ((f32[16,1,64]{2,1,0:T(1,128)}), f32[16,1,64]{2,1,0:T(1,128)S(1)}, u32[]{:S(2)}, u32[]{:S(2)}) async-start(f32[16,1,64]{2,1,0:T(1,128)} %all_to_all.16), calls=%async_computation | async-start | bytes 16384 | tf_op jit(solution)/shard_map/all_to_all | solution.py:41
  59.9 0.2 exponential_reduce_fusion.1
  60.1 0.7 all_to_all.18
  60.8 4.2 %all-gather.3 = f32[2,1,128]{2,1,0:T(1,128)S(1)} all-gather(f32[1,1,128]{2,1,0:T(1,128)S(1)} %bitcast.48), channel_id=3, replica_groups=mesh['batch'=16,'rep'=2] {'rep'}, dimensions={0}, use_global_device_ids=true | all-gather | bytes 1536 | tf_op jit(solution)/shard_map/all_gather | solution.py:8
  65.0 4.2 %all-gather.2 = f32[2,1,128]{2,1,0:T(1,128)S(1)} all-gather(f32[1,1,128]{2,1,0:T(1,128)S(1)} %bitcast.47), channel_id=2, replica_groups=mesh['batch'=16,'rep'=2] {'rep'}, dimensions={0}, use_global_device_ids=true | all-gather | bytes 1536 | tf_op jit(solution)/shard_map/all_gather | solution.py:8
  69.3 0.0 all-to-all-done
  69.3 6.0 %all-to-all-start.1 = ((f32[16,1,64]{2,1,0:T(1,128)}), f32[16,1,64]{2,1,0:T(1,128)S(1)}, u32[]{:S(2)}, u32[]{:S(2)}) async-start(f32[16,1,64]{2,1,0:T(1,128)} %all_to_all.18), calls=%async_computation.1 | async-start | bytes 16384 | tf_op jit(solution)/shard_map/all_to_all | solution.py:48
  75.3 0.0 reduce-scatter.2.cloned.1.call-start
  75.4 4.0 %all-to-all-done.1 = f32[16,1,64]{2,1,0:T(1,128)S(1)} async-done(((f32[16,1,64]{2,1,0:T(1,128)}), f32[16,1,64]{2,1,0:T(1,128)S(1)}, u32[]{:S(2)}, u32[]{:S(2)}) %all-to-all-start.1) | async-done | bytes 4128 | tf_op jit(solution)/shard_map/all_to_all | solution.py:48
  79.4 0.1 fusion.25
  79.5 23.2 %all-reduce = f32[1024]{0:T(1024)S(1)} all-reduce(f32[1024]{0:T(1024)S(1)} %get-tuple-element.22), channel_id=1, replica_groups=mesh['batch'=16,'rep'=2] {'batch'}, use_global_device_ids=true, to_apply=%add | all-reduce | flops 1024 | bytes 8192
  102.7 3.0 %convolution_multiply_fusion.1 = f32[128,1024]{1,0:T(8,128)} fusion(bf16[1024,1024]{1,0:T(8,128)(2,1)} %all-gather.8.cloned.1.call-done, f32[128,1024]{1,0:T(8,128)S(1)} %get-tuple-element.24, s32[1024]{0:T(1024)S(1)} %iota_subtract_fusion, f32[1024]{0:T(1024)S(1)} %all-reduce, f32[128]{0:T(128)S(1)} %log_add_fusion.1, f32[]{:T(128)S(6)} %mul.86, ...), kind=kOutput, calls=%fused_computation.2 | convolution fusion | flops 269746176 | bytes 3156996 | tf_op jit(solution)/shard_map/dot_general | solution.py:77
  105.7 0.0 reduce-scatter.2.cloned.1.call-update
  105.8 0.1 dynamic_slice.12
  105.9 0.8 gather_fusion
  106.7 0.7 subtract_reduce_fusion
  107.4 23.9 %all-gather.4 = f32[16,1,128]{2,1,0:T(1,128)S(1)} all-gather(f32[1,1,128]{2,1,0:T(1,128)S(1)} %bitcast.46), channel_id=1, replica_groups=mesh['batch'=16,'rep'=2] {'batch'}, dimensions={0}, use_global_device_ids=true | all-gather | bytes 8704 | tf_op jit(solution)/shard_map/all_gather | solution.py:80
  131.3 43.0 %psum.7 = f32[]{:T(128)} all-reduce(f32[]{:T(128)} %subtract_reduce_fusion), channel_id=1, replica_groups=mesh['batch'=16,'rep'=2] {'batch','rep'}, use_global_device_ids=true, to_apply=%region_7.8 | all-reduce | flops 1 | bytes 8 | tf_op jit(solution)/shard_map/psum | solution.py:66
  174.9 0.0 all-gather.10.cloned.1.call-done
  175.0 0.0 copy-done
  175.0 6.4 %convolution_multiply_fusion.3 = f32[64,1024]{1,0:T(8,128)} fusion(bf16[2048,1024]{1,0:T(8,128)(2,1)} %all-gather.10.cloned.1.call-done, bf16[64,1024]{1,0:T(8,128)(2,1)S(1)} %copy-done, s32[64]{0:T(128)S(1)} %iota_add_fusion, f32[2048]{0:T(1024)S(1)} %bitcast.45, f32[64]{0:T(128)S(1)} %get-tuple-element.23, f32[]{:T(128)} %bitcast.42, f32[]{:T(128)S(6)} %mul.86), kind=kOutput, calls=%fused_computation.4 | convolution fusion | flops 537985024 | bytes 4596232 | tf_op jit(solution)/shard_map/dot_general | solution.py:94
  181.4 0.0 reduce-scatter.2.cloned.1.call-done
  (9 shorter events, 0.1 us)
Async XLA Ops:
  7.2 43.6 %all-gather.8.cloned.1.call-start = ((), (), s32[]{:S(2)}) async-start(), calls=%async_computation.3 | async-start | bytes 2228224 | tf_op jit(solution)/shard_map/all_gather | solution.py:30
  7.9 167.1 %copy-start = (bf16[64,1024]{1,0:T(8,128)(2,1)S(1)}, bf16[64,1024]{1,0:T(8,128)(2,1)}, u32[]{:S(2)}) copy-start(bf16[64,1024]{1,0:T(8,128)(2,1)} %param.4) | copy-start | bytes 393220
  7.9 167.1 %all-gather.10.cloned.1.call-start = ((), (), s32[]{:S(2)}) async-start(), calls=%async_computation.5 | async-start | bytes 4456448 | tf_op jit(solution)/shard_map/all_gather | solution.py:82
  54.1 15.2 %all-to-all-start = ((f32[16,1,64]{2,1,0:T(1,128)}), f32[16,1,64]{2,1,0:T(1,128)S(1)}, u32[]{:S(2)}, u32[]{:S(2)}) async-start(f32[16,1,64]{2,1,0:T(1,128)} %all_to_all.16), calls=%async_computation | async-start | bytes 16384 | tf_op jit(solution)/shard_map/all_to_all | solution.py:41
  69.3 10.1 %all-to-all-start.1 = ((f32[16,1,64]{2,1,0:T(1,128)}), f32[16,1,64]{2,1,0:T(1,128)S(1)}, u32[]{:S(2)}, u32[]{:S(2)}) async-start(f32[16,1,64]{2,1,0:T(1,128)} %all_to_all.18), calls=%async_computation.1 | async-start | bytes 16384 | tf_op jit(solution)/shard_map/all_to_all | solution.py:48
  75.3 106.1 %reduce-scatter.2.cloned.1.call-start = ((), (), s32[]{:S(2)}) async-start(), calls=%async_computation.4 | async-start | bytes 786432 | tf_op jit(solution)/shard_map/reduce_scatter | solution.py:79
Sparse Core Ops, SparseCore 0:
  10.1 40.6 all-gather.7
  52.9 50.6 all-gather.9
  106.4 20.2 reduce-scatter.1
where the time goes:
time: 189 us
  blocking collectives  98.6 us (52%)
  waiting for transfers between devices  44.9 us (24%)
  between operations  16.9 us (9%)
  starting transfers between devices  12 us (6%)
  matrix products  12 us (6%)
  local copies, waits for them, and re-layouts  3.51 us (2%)
    psum x1, blocking collectives, body(): lax.psum(jnp.sum(own_rows + own_lse - 2.0 * own_diag), ('batch', 'rep'))  43 us
    all_gather x1, waiting for transfers between devices, body(): whole_text = lax.all_gather(text_embed, 'batch', axis=0, tiled=True)  39.5 us
    all_gather x1, blocking collectives, body(): all_rows_lse = lax.all_gather(row_lse, 'batch', axis=0, tiled=True)  23.9 us
    unnamed x1, blocking collectives  23.2 us
    all_gather x2, blocking collectives, merged(): pieces = jax.tree.map(lambda part: lax.all_gather(part, axis), value)  8.45 us
    dot_general x1, matrix products, body(): jnp.dot(weights_block, fragment, preferred_element_type=jnp.float32)  6.37 us
    all_to_all x1, starting transfers between devices, body(): lax.all_to_all(column_sum.reshape(batch_count, half_rows), 'batch', split...  6.02 us
    all_to_all x1, starting transfers between devices, body(): lax.all_to_all(column_max.reshape(batch_count, half_rows), 'batch', split...  5.83 us
  transfers between devices with their start and end apart: 5, of which 2 were waited for; matrix products, arithmetic and copies ran while one was open for 8% of the time, Pallas kernels for 0%

commit v1 on v0

--- a/solution.py
+++ b/solution.py
@@ -27,7 +27,14 @@
     batch_count = lax.axis_size("batch")
     batch_index = lax.axis_index("batch")
     rep_index = lax.axis_index("rep")
-    whole_text = lax.all_gather(text_embed, "batch", axis=0, tiled=True)
+    ring = [text_embed]
+    for hop in range(15):
+        ring.append(lax.ppermute(ring[-1], "batch", [(dev, (dev + 1) % 16) for dev in range(16)]))
+    whole_text = jnp.roll(
+        jnp.concatenate(ring[::-1], axis=0),
+        (lax.axis_index("batch") + 1) * ring[0].shape[0],
+        axis=0,
+    )
     scores = scale_value * lax.dot_general(
         image_embed, whole_text, (((1,), (1,)), ((), ())), preferred_element_type=jnp.float32
     )

time: 189 us -> 262 us (1.39)
  starting transfers between devices: 12 us -> 96.3 us
  waiting for transfers between devices: 44.9 us -> 30 us
    ppermute x0 -> x15, starting transfers between devices: none -> 60.1 us  [body(): lax.ppermute(ring[-1], 'batch', [(dev, (dev + 1) % 16) for dev in range(1...]
    all_gather x1 -> x0, waiting for transfers between devices: 39.5 us -> none  [body(): whole_text = lax.all_gather(text_embed, 'batch', axis=0, tiled=True)]
    ppermute x0 -> x15, waiting for transfers between devices: none -> 25.4 us  [body(): lax.ppermute(ring[-1], 'batch', [(dev, (dev + 1) % 16) for dev in range(1...]
    all_to_all x1, starting transfers between devices: 5.83 us -> 30.1 us  [body(): lax.all_to_all(column_max.reshape(batch_count, half_rows), 'batch', split...]
  transfers between devices with their start and end apart: 5 -> 19, of which waited for: 2 -> 15; matrix products, arithmetic and copies ran while one was open for 8% -> 6% of each run, Pallas kernels for 0% -> 0%
where the time goes in v1:
time: 262 us; the launch traced here: 261 us
  blocking collectives  97.7 us (37%)
  starting transfers between devices  96.3 us (37%)
  waiting for transfers between devices  30 us (11%)
  between operations  18.9 us (7%)
  matrix products  11.3 us (4%)
  local copies, waits for them, and re-layouts  5.83 us (2%)
    ppermute x15, starting transfers between devices, body(): lax.ppermute(ring[-1], 'batch', [(dev, (dev + 1) % 16) for dev in range(1...  60.1 us
    psum x1, blocking collectives, body(): lax.psum(jnp.sum(own_rows + own_lse - 2.0 * own_diag), ('batch', 'rep'))  43 us
    all_to_all x1, starting transfers between devices, body(): lax.all_to_all(column_max.reshape(batch_count, half_rows), 'batch', split...  30.1 us
    ppermute x15, waiting for transfers between devices, body(): lax.ppermute(ring[-1], 'batch', [(dev, (dev + 1) % 16) for dev in range(1...  25.4 us
    all_gather x1, blocking collectives, body(): all_rows_lse = lax.all_gather(row_lse, 'batch', axis=0, tiled=True)  24.8 us
    unnamed x1, blocking collectives  21.5 us
    all_gather x2, blocking collectives, merged(): pieces = jax.tree.map(lambda part: lax.all_gather(part, axis), value)  8.45 us
    dot_general x1, matrix products, body(): jnp.dot(weights_block, fragment, preferred_element_type=jnp.float32)  6.37 us
  transfers between devices with their start and end apart: 19, of which 15 were waited for; matrix products, arithmetic and copies ran while one was open for 6% of the time, Pallas kernels for 0%

profile of v1, /device:TPU:12, one launch (start us, length us, event | category | flops | bytes accessed | tf_op | source)
XLA Modules:
  0.0 261.4 jit_solution(16765510096461548667)
XLA Ops:
  8.1 0.7 all-gather.7.cloned.1.call-update
  8.8 4.6 %collective-permute-done = bf16[64,1024]{1,0:T(8,128)(2,1)S(1)} collective-permute-done((bf16[64,1024]{1,0:T(8,128)(2,1)}, bf16[64,1024]{1,0:T(8,128)(2,1)S(1)}, u32[]{:S(2)}, u32[]{:S(2)}) %collective-permute-start) | collective-permute-done | bytes 131104 | tf_op jit(solution)/shard_map/ppermute | solution.py:32
  13.4 4.4 %collective-permute-done.1 = bf16[64,1024]{1,0:T(8,128)(2,1)S(1)} collective-permute-done((bf16[64,1024]{1,0:T(8,128)(2,1)S(1)}, bf16[64,1024]{1,0:T(8,128)(2,1)S(1)}, u32[]{:S(2)}, u32[]{:S(2)}) %collective-permute-start.1) | collective-permute-done | bytes 131104 | tf_op jit(solution)/shard_map/ppermute | solution.py:32
  17.8 0.1 collective-permute-start.2
  17.9 4.9 %collective-permute-done.2 = bf16[64,1024]{1,0:T(8,128)(2,1)S(1)} collective-permute-done((bf16[64,1024]{1,0:T(8,128)(2,1)S(1)}, bf16[64,1024]{1,0:T(8,128)(2,1)S(1)}, u32[]{:S(2)}, u32[]{:S(2)}) %collective-permute-start.2) | collective-permute-done | bytes 131104 | tf_op jit(solution)/shard_map/ppermute | solution.py:32
  22.7 2.9 %collective-permute-start.3 = (bf16[64,1024]{1,0:T(8,128)(2,1)S(1)}, bf16[64,1024]{1,0:T(8,128)(2,1)S(1)}, u32[]{:S(2)}, u32[]{:S(2)}) collective-permute-start(bf16[64,1024]{1,0:T(8,128)(2,1)S(1)} %collective-permute-done.2), channel_id=1, source_target_pairs={{0,2},{2,4},{4,6},{6,8},{8,10},{10,12},{12,14},{14,16},{16,18},{18... | collective-permute-start | bytes 393224 | tf_op jit(solution)/shard_map/ppermute | solution.py:32
  25.6 1.5 collective-permute-done.3
  27.1 5.9 %collective-permute-start.4 = (bf16[64,1024]{1,0:T(8,128)(2,1)S(1)}, bf16[64,1024]{1,0:T(8,128)(2,1)S(1)}, u32[]{:S(2)}, u32[]{:S(2)}) collective-permute-start(bf16[64,1024]{1,0:T(8,128)(2,1)S(1)} %collective-permute-done.3), channel_id=1, source_target_pairs={{0,2},{2,4},{4,6},{6,8},{8,10},{10,12},{12,14},{14,16},{16,18},{18... | collective-permute-start | bytes 393224 | tf_op jit(solution)/shard_map/ppermute | solution.py:32
  33.0 1.0 collective-permute-done.4
  34.0 4.3 %collective-permute-start.5 = (bf16[64,1024]{1,0:T(8,128)(2,1)S(1)}, bf16[64,1024]{1,0:T(8,128)(2,1)S(1)}, u32[]{:S(2)}, u32[]{:S(2)}) collective-permute-start(bf16[64,1024]{1,0:T(8,128)(2,1)S(1)} %collective-permute-done.4), channel_id=1, source_target_pairs={{0,2},{2,4},{4,6},{6,8},{8,10},{10,12},{12,14},{14,16},{16,18},{18... | collective-permute-start | bytes 393224 | tf_op jit(solution)/shard_map/ppermute | solution.py:32
  38.3 1.0 collective-permute-done.5
  39.3 9.4 %collective-permute-start.6 = (bf16[64,1024]{1,0:T(8,128)(2,1)S(1)}, bf16[64,1024]{1,0:T(8,128)(2,1)S(1)}, u32[]{:S(2)}, u32[]{:S(2)}) collective-permute-start(bf16[64,1024]{1,0:T(8,128)(2,1)S(1)} %collective-permute-done.5), channel_id=1, source_target_pairs={{0,2},{2,4},{4,6},{6,8},{8,10},{10,12},{12,14},{14,16},{16,18},{18... | collective-permute-start | bytes 393224 | tf_op jit(solution)/shard_map/ppermute | solution.py:32
  48.7 1.0 collective-permute-done.6
  49.7 5.7 %collective-permute-start.7 = (bf16[64,1024]{1,0:T(8,128)(2,1)S(1)}, bf16[64,1024]{1,0:T(8,128)(2,1)S(1)}, u32[]{:S(2)}, u32[]{:S(2)}) collective-permute-start(bf16[64,1024]{1,0:T(8,128)(2,1)S(1)} %collective-permute-done.6), channel_id=1, source_target_pairs={{0,2},{2,4},{4,6},{6,8},{8,10},{10,12},{12,14},{14,16},{16,18},{18... | collective-permute-start | bytes 393224 | tf_op jit(solution)/shard_map/ppermute | solution.py:32
  55.4 1.2 collective-permute-done.7
  56.5 5.5 %collective-permute-start.8 = (bf16[64,1024]{1,0:T(8,128)(2,1)S(1)}, bf16[64,1024]{1,0:T(8,128)(2,1)S(1)}, u32[]{:S(2)}, u32[]{:S(2)}) collective-permute-start(bf16[64,1024]{1,0:T(8,128)(2,1)S(1)} %collective-permute-done.7), channel_id=1, source_target_pairs={{0,2},{2,4},{4,6},{6,8},{8,10},{10,12},{12,14},{14,16},{16,18},{18... | collective-permute-start | bytes 393224 | tf_op jit(solution)/shard_map/ppermute | solution.py:32
  62.1 1.0 collective-permute-done.8
  63.0 4.7 %collective-permute-start.9 = (bf16[64,1024]{1,0:T(8,128)(2,1)S(1)}, bf16[64,1024]{1,0:T(8,128)(2,1)S(1)}, u32[]{:S(2)}, u32[]{:S(2)}) collective-permute-start(bf16[64,1024]{1,0:T(8,128)(2,1)S(1)} %collective-permute-done.8), channel_id=1, source_target_pairs={{0,2},{2,4},{4,6},{6,8},{8,10},{10,12},{12,14},{14,16},{16,18},{18... | collective-permute-start | bytes 393224 | tf_op jit(solution)/shard_map/ppermute | solution.py:32
  67.7 1.0 collective-permute-done.9
  68.7 4.3 %collective-permute-start.10 = (bf16[64,1024]{1,0:T(8,128)(2,1)S(1)}, bf16[64,1024]{1,0:T(8,128)(2,1)S(1)}, u32[]{:S(2)}, u32[]{:S(2)}) collective-permute-start(bf16[64,1024]{1,0:T(8,128)(2,1)S(1)} %collective-permute-done.9), channel_id=1, source_target_pairs={{0,2},{2,4},{4,6},{6,8},{8,10},{10,12},{12,14},{14,16},{16,18},{18... | collective-permute-start | bytes 393224 | tf_op jit(solution)/shard_map/ppermute | solution.py:32
  73.0 1.0 collective-permute-done.10
  74.0 4.3 %collective-permute-start.11 = (bf16[64,1024]{1,0:T(8,128)(2,1)S(1)}, bf16[64,1024]{1,0:T(8,128)(2,1)S(1)}, u32[]{:S(2)}, u32[]{:S(2)}) collective-permute-start(bf16[64,1024]{1,0:T(8,128)(2,1)S(1)} %collective-permute-done.10), channel_id=1, source_target_pairs={{0,2},{2,4},{4,6},{6,8},{8,10},{10,12},{12,14},{14,16},{16,18},{18... | collective-permute-start | bytes 393224 | tf_op jit(solution)/shard_map/ppermute | solution.py:32
  78.3 1.0 collective-permute-done.11
  79.3 4.3 %collective-permute-start.12 = (bf16[64,1024]{1,0:T(8,128)(2,1)S(1)}, bf16[64,1024]{1,0:T(8,128)(2,1)S(1)}, u32[]{:S(2)}, u32[]{:S(2)}) collective-permute-start(bf16[64,1024]{1,0:T(8,128)(2,1)S(1)} %collective-permute-done.11), channel_id=1, source_target_pairs={{0,2},{2,4},{4,6},{6,8},{8,10},{10,12},{12,14},{14,16},{16,18},{18... | collective-permute-start | bytes 393224 | tf_op jit(solution)/shard_map/ppermute | solution.py:32
  83.6 1.0 collective-permute-done.12
  84.6 4.3 %collective-permute-start.13 = (bf16[64,1024]{1,0:T(8,128)(2,1)S(1)}, bf16[64,1024]{1,0:T(8,128)(2,1)S(1)}, u32[]{:S(2)}, u32[]{:S(2)}) collective-permute-start(bf16[64,1024]{1,0:T(8,128)(2,1)S(1)} %collective-permute-done.12), channel_id=1, source_target_pairs={{0,2},{2,4},{4,6},{6,8},{8,10},{10,12},{12,14},{14,16},{16,18},{18... | collective-permute-start | bytes 393224 | tf_op jit(solution)/shard_map/ppermute | solution.py:32
  88.9 1.0 collective-permute-done.13
  89.9 4.3 %collective-permute-start.14 = (bf16[64,1024]{1,0:T(8,128)(2,1)S(1)}, bf16[64,1024]{1,0:T(8,128)(2,1)S(1)}, u32[]{:S(2)}, u32[]{:S(2)}) collective-permute-start(bf16[64,1024]{1,0:T(8,128)(2,1)S(1)} %collective-permute-done.13), channel_id=1, source_target_pairs={{0,2},{2,4},{4,6},{6,8},{8,10},{10,12},{12,14},{14,16},{16,18},{18... | collective-permute-start | bytes 393224 | tf_op jit(solution)/shard_map/ppermute | solution.py:32
  94.9 1.2 dynamic-slice.4
  97.4 2.0 copy-done
  99.4 0.8 fusion.38
  100.2 0.7 all_to_all.16
  100.9 30.1 %all-to-all-start = ((f32[16,1,64]{2,1,0:T(1,128)}), f32[16,1,64]{2,1,0:T(1,128)S(1)}, u32[]{:S(2)}, u32[]{:S(2)}) async-start(f32[16,1,64]{2,1,0:T(1,128)} %all_to_all.16), calls=%async_computation | async-start | bytes 16384 | tf_op jit(solution)/shard_map/all_to_all | solution.py:48
  131.0 0.4 exponential_reduce_fusion.1
  131.3 0.7 all_to_all.18
  132.0 4.2 %all-gather.3 = f32[2,1,128]{2,1,0:T(1,128)S(1)} all-gather(f32[1,1,128]{2,1,0:T(1,128)S(1)} %bitcast.53), channel_id=3, replica_groups=mesh['batch'=16,'rep'=2] {'rep'}, dimensions={0}, use_global_device_ids=true | all-gather | bytes 1536 | tf_op jit(solution)/shard_map/all_gather | solution.py:8
  136.2 4.2 %all-gather.2 = f32[2,1,128]{2,1,0:T(1,128)S(1)} all-gather(f32[1,1,128]{2,1,0:T(1,128)S(1)} %bitcast.52), channel_id=2, replica_groups=mesh['batch'=16,'rep'=2] {'rep'}, dimensions={0}, use_global_device_ids=true | all-gather | bytes 1536 | tf_op jit(solution)/shard_map/all_gather | solution.py:8
  140.5 6.1 %all-to-all-start.1 = ((f32[16,1,64]{2,1,0:T(1,128)}), f32[16,1,64]{2,1,0:T(1,128)S(1)}, u32[]{:S(2)}, u32[]{:S(2)}) async-start(f32[16,1,64]{2,1,0:T(1,128)} %all_to_all.18), calls=%async_computation.1 | async-start | bytes 16384 | tf_op jit(solution)/shard_map/all_to_all | solution.py:55
  146.6 3.9 %all-to-all-done.1 = f32[16,1,64]{2,1,0:T(1,128)S(1)} async-done(((f32[16,1,64]{2,1,0:T(1,128)}), f32[16,1,64]{2,1,0:T(1,128)S(1)}, u32[]{:S(2)}, u32[]{:S(2)}) %all-to-all-start.1) | async-done | bytes 4128 | tf_op jit(solution)/shard_map/all_to_all | solution.py:55
  150.6 0.1 fusion.39
  150.7 21.5 %all-reduce = f32[1024]{0:T(1024)S(1)} all-reduce(f32[1024]{0:T(1024)S(1)} %get-tuple-element.22), channel_id=1, replica_groups=mesh['batch'=16,'rep'=2] {'batch'}, use_global_device_ids=true, to_apply=%add | all-reduce | flops 1024 | bytes 8192
  172.2 4.1 %fusion.7 = f32[128,1024]{1,0:T(8,128)} fusion(bf16[2048,1024]{1,0:T(8,128)(2,1)} %copy-done, s32[]{:T(128)S(6)} %select_n.25, f32[1024,128]{1,0:T(8,128)S(1)} %get-tuple-element.24, s32[128]{0:T(128)S(1)} %iota_subtract_fusion.1, f32[1024]{0:T(1024)S(1)} %all-reduce, f32[128]{0:T(128)S(1)} %log_add_fusion.1, f32[]{:T(128)S(6)} %mul.91, ...), kind=kOutput, calls=%fused_computation.7 | convolution fusion | flops 269746176 | bytes 3157000 | tf_op jit(solution)/shard_map/dot_general | solution.py:84
  176.4 0.1 dynamic-slice_bitcast_fusion
  176.5 0.8 gather_fusion
  177.3 0.7 subtract_reduce_fusion
  178.0 24.8 %all-gather.4 = f32[16,1,128]{2,1,0:T(1,128)S(1)} all-gather(f32[1,1,128]{2,1,0:T(1,128)S(1)} %bitcast.51), channel_id=1, replica_groups=mesh['batch'=16,'rep'=2] {'batch'}, dimensions={0}, use_global_device_ids=true | all-gather | bytes 8704 | tf_op jit(solution)/shard_map/all_gather | solution.py:87
  202.7 43.0 %psum.7 = f32[]{:T(128)} all-reduce(f32[]{:T(128)} %subtract_reduce_fusion), channel_id=1, replica_groups=mesh['batch'=16,'rep'=2] {'batch','rep'}, use_global_device_ids=true, to_apply=%region_7.8 | all-reduce | flops 1 | bytes 8 | tf_op jit(solution)/shard_map/psum | solution.py:73
  246.4 6.4 %convolution_multiply_fusion.1 = f32[64,1024]{1,0:T(8,128)} fusion(bf16[2048,1024]{1,0:T(8,128)(2,1)} %all-gather.7.cloned.1.call-done, bf16[64,1024]{1,0:T(8,128)(2,1)S(1)} %copy-done.1, s32[64]{0:T(128)S(1)} %iota_add_fusion, f32[2048]{0:T(1024)S(1)} %bitcast.50, f32[64]{0:T(128)S(1)} %get-tuple-element.23, f32[]{:T(128)} %bitcast.47, f32[]{:T(128)S(6)} %mul.91), kind=kOutput, calls=%fused_computation.8 | convolution fusion | flops 537985024 | bytes 4596232 | tf_op jit(solution)/shard_map/dot_general | solution.py:101
  (55 shorter events, 0.7 us)
Async XLA Ops:
  8.0 89.1 %copy-start.1 = (bf16[64,1024]{1,0:T(8,128)(2,1)S(1)}, bf16[64,1024]{1,0:T(8,128)(2,1)}, u32[]{:S(2)}) copy-start(bf16[64,1024]{1,0:T(8,128)(2,1)} %param.4) | copy-start | bytes 393220
  8.0 238.4 %all-gather.7.cloned.1.call-start = ((), (), s32[]{:S(2)}) async-start(), calls=%async_computation.4 | async-start | bytes 4456448 | tf_op jit(solution)/shard_map/all_gather | solution.py:89
  8.7 4.7 %collective-permute-start = (bf16[64,1024]{1,0:T(8,128)(2,1)}, bf16[64,1024]{1,0:T(8,128)(2,1)S(1)}, u32[]{:S(2)}, u32[]{:S(2)}) collective-permute-start(bf16[64,1024]{1,0:T(8,128)(2,1)} %param.4), channel_id=1, source_target_pairs={{0,2},{2,4},{4,6},{6,8},{8,10},{10,12},{12,14},{14,16},{16,18},{18... | collective-permute-start | bytes 393224 | tf_op jit(solution)/shard_map/ppermute | solution.py:32
  13.4 4.4 %collective-permute-start.1 = (bf16[64,1024]{1,0:T(8,128)(2,1)S(1)}, bf16[64,1024]{1,0:T(8,128)(2,1)S(1)}, u32[]{:S(2)}, u32[]{:S(2)}) collective-permute-start(bf16[64,1024]{1,0:T(8,128)(2,1)S(1)} %collective-permute-done), channel_id=1, source_target_pairs={{0,2},{2,4},{4,6},{6,8},{8,10},{10,12},{12,14},{14,16},{16,18},{18... | collective-permute-start | bytes 393224 | tf_op jit(solution)/shard_map/ppermute | solution.py:32
  17.8 4.9 %collective-permute-start.2 = (bf16[64,1024]{1,0:T(8,128)(2,1)S(1)}, bf16[64,1024]{1,0:T(8,128)(2,1)S(1)}, u32[]{:S(2)}, u32[]{:S(2)}) collective-permute-start(bf16[64,1024]{1,0:T(8,128)(2,1)S(1)} %collective-permute-done.1), channel_id=1, source_target_pairs={{0,2},{2,4},{4,6},{6,8},{8,10},{10,12},{12,14},{14,16},{16,18},{18... | collective-permute-start | bytes 393224 | tf_op jit(solution)/shard_map/ppermute | solution.py:32
  22.7 4.4 %collective-permute-start.3 = (bf16[64,1024]{1,0:T(8,128)(2,1)S(1)}, bf16[64,1024]{1,0:T(8,128)(2,1)S(1)}, u32[]{:S(2)}, u32[]{:S(2)}) collective-permute-start(bf16[64,1024]{1,0:T(8,128)(2,1)S(1)} %collective-permute-done.2), channel_id=1, source_target_pairs={{0,2},{2,4},{4,6},{6,8},{8,10},{10,12},{12,14},{14,16},{16,18},{18... | collective-permute-start | bytes 393224 | tf_op jit(solution)/shard_map/ppermute | solution.py:32
  27.1 6.9 %collective-permute-start.4 = (bf16[64,1024]{1,0:T(8,128)(2,1)S(1)}, bf16[64,1024]{1,0:T(8,128)(2,1)S(1)}, u32[]{:S(2)}, u32[]{:S(2)}) collective-permute-start(bf16[64,1024]{1,0:T(8,128)(2,1)S(1)} %collective-permute-done.3), channel_id=1, source_target_pairs={{0,2},{2,4},{4,6},{6,8},{8,10},{10,12},{12,14},{14,16},{16,18},{18... | collective-permute-start | bytes 393224 | tf_op jit(solution)/shard_map/ppermute | solution.py:32
  34.0 5.3 %collective-permute-start.5 = (bf16[64,1024]{1,0:T(8,128)(2,1)S(1)}, bf16[64,1024]{1,0:T(8,128)(2,1)S(1)}, u32[]{:S(2)}, u32[]{:S(2)}) collective-permute-start(bf16[64,1024]{1,0:T(8,128)(2,1)S(1)} %collective-permute-done.4), channel_id=1, source_target_pairs={{0,2},{2,4},{4,6},{6,8},{8,10},{10,12},{12,14},{14,16},{16,18},{18... | collective-permute-start | bytes 393224 | tf_op jit(solution)/shard_map/ppermute | solution.py:32
  39.3 10.4 %collective-permute-start.6 = (bf16[64,1024]{1,0:T(8,128)(2,1)S(1)}, bf16[64,1024]{1,0:T(8,128)(2,1)S(1)}, u32[]{:S(2)}, u32[]{:S(2)}) collective-permute-start(bf16[64,1024]{1,0:T(8,128)(2,1)S(1)} %collective-permute-done.5), channel_id=1, source_target_pairs={{0,2},{2,4},{4,6},{6,8},{8,10},{10,12},{12,14},{14,16},{16,18},{18... | collective-permute-start | bytes 393224 | tf_op jit(solution)/shard_map/ppermute | solution.py:32
  49.7 6.9 %collective-permute-start.7 = (bf16[64,1024]{1,0:T(8,128)(2,1)S(1)}, bf16[64,1024]{1,0:T(8,128)(2,1)S(1)}, u32[]{:S(2)}, u32[]{:S(2)}) collective-permute-start(bf16[64,1024]{1,0:T(8,128)(2,1)S(1)} %collective-permute-done.6), channel_id=1, source_target_pairs={{0,2},{2,4},{4,6},{6,8},{8,10},{10,12},{12,14},{14,16},{16,18},{18... | collective-permute-start | bytes 393224 | tf_op jit(solution)/shard_map/ppermute | solution.py:32
  56.5 6.5 %collective-permute-start.8 = (bf16[64,1024]{1,0:T(8,128)(2,1)S(1)}, bf16[64,1024]{1,0:T(8,128)(2,1)S(1)}, u32[]{:S(2)}, u32[]{:S(2)}) collective-permute-start(bf16[64,1024]{1,0:T(8,128)(2,1)S(1)} %collective-permute-done.7), channel_id=1, source_target_pairs={{0,2},{2,4},{4,6},{6,8},{8,10},{10,12},{12,14},{14,16},{16,18},{18... | collective-permute-start | bytes 393224 | tf_op jit(solution)/shard_map/ppermute | solution.py:32
  63.0 5.7 %collective-permute-start.9 = (bf16[64,1024]{1,0:T(8,128)(2,1)S(1)}, bf16[64,1024]{1,0:T(8,128)(2,1)S(1)}, u32[]{:S(2)}, u32[]{:S(2)}) collective-permute-start(bf16[64,1024]{1,0:T(8,128)(2,1)S(1)} %collective-permute-done.8), channel_id=1, source_target_pairs={{0,2},{2,4},{4,6},{6,8},{8,10},{10,12},{12,14},{14,16},{16,18},{18... | collective-permute-start | bytes 393224 | tf_op jit(solution)/shard_map/ppermute | solution.py:32
  68.7 5.3 %collective-permute-start.10 = (bf16[64,1024]{1,0:T(8,128)(2,1)S(1)}, bf16[64,1024]{1,0:T(8,128)(2,1)S(1)}, u32[]{:S(2)}, u32[]{:S(2)}) collective-permute-start(bf16[64,1024]{1,0:T(8,128)(2,1)S(1)} %collective-permute-done.9), channel_id=1, source_target_pairs={{0,2},{2,4},{4,6},{6,8},{8,10},{10,12},{12,14},{14,16},{16,18},{18... | collective-permute-start | bytes 393224 | tf_op jit(solution)/shard_map/ppermute | solution.py:32
  74.0 5.3 %collective-permute-start.11 = (bf16[64,1024]{1,0:T(8,128)(2,1)S(1)}, bf16[64,1024]{1,0:T(8,128)(2,1)S(1)}, u32[]{:S(2)}, u32[]{:S(2)}) collective-permute-start(bf16[64,1024]{1,0:T(8,128)(2,1)S(1)} %collective-permute-done.10), channel_id=1, source_target_pairs={{0,2},{2,4},{4,6},{6,8},{8,10},{10,12},{12,14},{14,16},{16,18},{18... | collective-permute-start | bytes 393224 | tf_op jit(solution)/shard_map/ppermute | solution.py:32
  79.3 5.3 %collective-permute-start.12 = (bf16[64,1024]{1,0:T(8,128)(2,1)S(1)}, bf16[64,1024]{1,0:T(8,128)(2,1)S(1)}, u32[]{:S(2)}, u32[]{:S(2)}) collective-permute-start(bf16[64,1024]{1,0:T(8,128)(2,1)S(1)} %collective-permute-done.11), channel_id=1, source_target_pairs={{0,2},{2,4},{4,6},{6,8},{8,10},{10,12},{12,14},{14,16},{16,18},{18... | collective-permute-start | bytes 393224 | tf_op jit(solution)/shard_map/ppermute | solution.py:32
  84.6 5.3 %collective-permute-start.13 = (bf16[64,1024]{1,0:T(8,128)(2,1)S(1)}, bf16[64,1024]{1,0:T(8,128)(2,1)S(1)}, u32[]{:S(2)}, u32[]{:S(2)}) collective-permute-start(bf16[64,1024]{1,0:T(8,128)(2,1)S(1)} %collective-permute-done.12), channel_id=1, source_target_pairs={{0,2},{2,4},{4,6},{6,8},{8,10},{10,12},{12,14},{14,16},{16,18},{18... | collective-permute-start | bytes 393224 | tf_op jit(solution)/shard_map/ppermute | solution.py:32
  89.9 6.9 %collective-permute-start.14 = (bf16[64,1024]{1,0:T(8,128)(2,1)S(1)}, bf16[64,1024]{1,0:T(8,128)(2,1)S(1)}, u32[]{:S(2)}, u32[]{:S(2)}) collective-permute-start(bf16[64,1024]{1,0:T(8,128)(2,1)S(1)} %collective-permute-done.13), channel_id=1, source_target_pairs={{0,2},{2,4},{4,6},{6,8},{8,10},{10,12},{12,14},{14,16},{16,18},{18... | collective-permute-start | bytes 393224 | tf_op jit(solution)/shard_map/ppermute | solution.py:32
  96.8 2.6 %copy-start.2 = (bf16[128,1024]{1,0:T(8,128)(2,1)S(1)}, bf16[128,1024]{1,0:T(8,128)(2,1)}, u32[]{:S(2)}) copy-start(bf16[128,1024]{1,0:T(8,128)(2,1)} %param.3) | copy-start | bytes 786436
  97.4 2.0 copy-start
  100.9 39.6 %all-to-all-start = ((f32[16,1,64]{2,1,0:T(1,128)}), f32[16,1,64]{2,1,0:T(1,128)S(1)}, u32[]{:S(2)}, u32[]{:S(2)}) async-start(f32[16,1,64]{2,1,0:T(1,128)} %all_to_all.16), calls=%async_computation | async-start | bytes 16384 | tf_op jit(solution)/shard_map/all_to_all | solution.py:48
  140.5 10.1 %all-to-all-start.1 = ((f32[16,1,64]{2,1,0:T(1,128)}), f32[16,1,64]{2,1,0:T(1,128)S(1)}, u32[]{:S(2)}, u32[]{:S(2)}) async-start(f32[16,1,64]{2,1,0:T(1,128)} %all_to_all.18), calls=%async_computation.1 | async-start | bytes 16384 | tf_op jit(solution)/shard_map/all_to_all | solution.py:55
  146.5 106.3 %reduce-scatter.2.cloned.1.call-start = ((), (), s32[]{:S(2)}) async-start(), calls=%async_computation.3 | async-start | bytes 786432 | tf_op jit(solution)/shard_map/reduce_scatter | solution.py:86
Sparse Core Ops, SparseCore 0:
  11.0 54.1 all-gather.6
Sparse Core Ops, SparseCore 1:
  176.4 21.6 reduce-scatter.1
